TPU v7x, 16 devices: a whole 2x2x2 slice. The times are simulated.
16 devices in a mesh: yz: 4 (over z, y), x: 4 (over x, core).
Axes of the slice: x: 2, y: 2, z: 2, core: 2. Of those that a mesh axis runs over, the one named last changes fastest.
Arguments:
- h: bfloat16 [128, 2048], P(None, ('x', 'yz'))
- g: bfloat16 [2, 2048], P(None, ('x', 'yz'))
- wq: bfloat16 [2, 2048, 2048], P(None, 'x', 'yz')
- wk: bfloat16 [2, 2048, 2048], P(None, 'x', 'yz')
- wv: bfloat16 [2, 2048, 2048], P(None, 'x', 'yz')
- w_in: bfloat16 [2, 2048, 8192], P(None, 'x', 'yz')
- wo: bfloat16 [2, 2048, 2048], P(None, 'yz', 'x')
- w_out: bfloat16 [2, 8192, 2048], P(None, 'yz', 'x')
- k_cache: bfloat16 [2, 128, 16, 512, 128], P(None, None, ('yz', 'x'))
- v_cache: bfloat16 [2, 128, 16, 512, 128], P(None, None, ('yz', 'x'))
- lens: int32 [128], replicated
Outputs:
- output 1: bfloat16 [128, 2048], P(None, ('x', 'yz'))
- output 2: bfloat16 [2, 128, 16, 128], P(None, None, ('yz', 'x'))
- output 3: bfloat16 [2, 128, 16, 128], P(None, None, ('yz', 'x'))
All inputs are finite; a program needn't handle non-finite values.
Results may differ from a plain program's by a relative error of at most 0.0191147.
Values are sent between devices in bfloat16 or wider.
A program may use at most 1 GiB of HBM per device.

v0:
```python
import functools

import jax
import jax.numpy as jnp
import numpy as np
from jax import lax
from jax.experimental import pallas as pl
from jax.experimental.pallas import tpu as pltpu
from jax.sharding import PartitionSpec as P

EPS = 1e-6
MESH = pl.DeviceIdType.MESH
F32 = jnp.float32
BF16 = jnp.bfloat16

L = 2
B = 128
D = 128
S = 512
NX = 4
NY = 4
E = 2048
G = 16
NG = B // G


KINDS = {k: n for n, k in enumerate(("s", "h", "q", "kv", "kvx", "u", "ux", "f", "o", "y"))}
SENDS = {"s": 0, "h": 1, "q": 0, "kv": 1, "kvx": 1, "u": 2, "ux": 2, "f": 1, "o": 0, "y": 0}
ORDER = ("IN*0 SQA0 SQB0 JN*0 XA0 RKVA0 XA0 RUA0 XA0 XA0 QA0 QKA0 QKA0 RKVB0 RUB0 SMA0 PVA0 KVA0 SOA0 RUB0 QB0 QKB0 QKB0 "
         "FA0 SMB0 PVB0 KVB0 SOB0 MLPA0 OUTA0 XA1 FB0 XA1 XA1 MLPB0 OUTB0 XA1 HA0 XB1 LVA0 XB1 XB1 LVB0 XB1 HB0 INA1 SQA1 JNA1 "
         "RKVA1 RUA1 INB1 SQB1 RUA1 JNB1 QA1 QKA1 QKA1 RKVB1 RUB1 SMA1 PVA1 KVA1 SOA1 QB1 QKB1 QKB1 SMB1 PVB1 KVB1 SOB1 FA1 "
         "MLPA1 FB1 OUTA1 MLPB1 OUTB1 HA1 HB1").split()


def _dot(a, b):
    return jnp.dot(a, b, preferred_element_type=F32)


def _dot_t(a, b):
    return lax.dot_general(a, b, (((1,), (1,)), ((), ())), preferred_element_type=F32)


def _kernel(nch, h_in, g_in, wq_in, wk_in, wv_in, win_in, wo_in, wout_in, kc_in, vc_in, lens_in, inv_in,
            h_out, k_out, v_out,
            kbuf, vbuf, wqkv, win, wo, wout, gg, lrow, inv, cosb, sinb, lenb,
            hg, ssb, qf, qb, qr, pf, pb, rq, sf, sb, xr, uf, ub, ur, usf, usb, ux, fb, og, zf, zb, zr,
            xbuf, qv, obuf, sbuf, pbuf, mbuf, dbuf,
            sem_in, sem_w, sem_k, sem_v, g_sem, send_sem, recv_sem):
    R = B // nch
    xi = lax.axis_index("x")
    yi = lax.axis_index("yz")
    c = lax.rem(xi, 2)
    xc = lax.div(xi, 2)
    partner = xi + 1 - 2 * c
    across = lax.rem(xi + 2, NX)
    open_sends, regions = {}, {}

    def exchange(kind, l, ch, copies, region, first=True):
        ss, rs = send_sem.at[SENDS[kind], ch], recv_sem.at[KINDS[kind], ch]
        if first:
            drain(SENDS[kind], ch)
        for src, dst, dev in copies:
            pltpu.make_async_remote_copy(src_ref=src, dst_ref=dst, send_sem=ss, recv_sem=rs,
                                         device_id={"x": xi, "yz": yi, **dev}, device_id_type=MESH).start()
        open_sends[SENDS[kind], ch] = regions[kind, ch] = region

    def drain(n, ch):
        region = open_sends.pop((n, ch), None)
        if region is not None:
            pltpu.make_async_copy(region, region, send_sem.at[n, ch]).wait()

    def arrived(kind, ch):
        region = regions[kind, ch]
        with jax.named_scope(f"w_{kind}_{ch}"):
            pltpu.make_async_copy(region, region, recv_sem.at[KINDS[kind], ch]).wait()

    def load(src, dst, sem):
        cp = pltpu.make_async_copy(src, dst, sem)
        cp.start()
        return cp

    in_h = load(h_in, hg.at[0, yi], sem_in.at[0])
    in_g = load(g_in, gg.at[yi], sem_in.at[1])
    in_l = load(lens_in, lrow, sem_in.at[2])
    in_i = load(inv_in, inv, sem_in.at[3])

    def load_first(l):
        for n, w in enumerate((wq_in, wk_in, wv_in)):
            load(w.at[l], wqkv.at[l, n], sem_w.at[0])
        load(win_in.at[l], win.at[l], sem_w.at[1])

    def load_second(l):
        load(wo_in.at[l], wo.at[l], sem_w.at[2])
        load(wout_in.at[l], wout.at[l], sem_w.at[3])

    def need_w(l, n):
        ref = (wqkv, win, wo, wout)[n].at[l]
        pltpu.make_async_copy(ref, ref, sem_w.at[n]).wait()

    load_first(0)

    barrier = pltpu.get_barrier_semaphore()
    for dx in range(NX):
        for dy in range(NY):
            if dx or dy:
                pl.semaphore_signal(barrier, inc=1, device_id={"yz": lax.rem(yi + dy, NY), "x": lax.rem(xi + dx, NX)},
                                    device_id_type=MESH)

    eye = (lax.broadcasted_iota(jnp.int32, (R, B), 0) == lax.broadcasted_iota(jnp.int32, (R, B), 1))

    def stats(l, ch, hb):
        col = jnp.sum(hb * hb, axis=1, keepdims=True)
        ssb[l, 0, ch] = jnp.sum(jnp.where(eye, col, 0.0), axis=0, keepdims=True)

    def send_h(l, ch, rows, chs):
        exchange("s", l, ch,
                 [(ssb.at[l, 0, chs], ssb.at[l, dx * NY + dy, chs],
                   {"x": lax.rem(xi + dx, NX), "yz": lax.rem(yi + dy, NY)})
                  for dx in (2, 1, 3, 0) for dy in (3, 1, 2, 0) if dx or dy],
                 ssb.at[l, pl.ds(1, NX * NY - 1), chs])
        exchange("h", l, ch,
                 [(hg.at[l, yi, rows], hg.at[l, yi, rows], {"yz": lax.rem(yi + d, NY)}) for d in (3, 1, 2)],
                 hg.at[l, pl.ds(0, NY - 1), rows])

    in_h.wait()
    in_g.wait()
    for ch in range(nch):
        stats(0, ch, hg[0, yi, pl.ds(ch * R, R), :].astype(F32))
    with jax.named_scope('barrier_wait'):
        pl.semaphore_wait(barrier, NX * NY - 1)
    send_h(0, 0, pl.ds(0, B), pl.ds(0, nch))
    for d in (1, 2, 3):
        pltpu.make_async_remote_copy(src_ref=gg.at[yi], dst_ref=gg.at[yi], send_sem=g_sem.at[0], recv_sem=g_sem.at[1],
                                     device_id={"x": xi, "yz": lax.rem(yi + d, NY)}, device_id_type=MESH).start()

    def load_cache(src, buf, sem, l, ch):
        for grp in range(ch * gpc, (ch + 1) * gpc):
            seqs = pl.ds(grp * G, G)
            load(src.at[l, seqs], buf.at[seqs], sem.at[ch])

    def need_cache(buf, sem, ch):
        ref = buf.at[pl.ds(ch * R, R)]
        pltpu.make_async_copy(ref, ref, sem.at[ch]).wait()

    gpc = NG // nch
    for ch in range(nch):
        load_cache(kc_in, kbuf, sem_k, 0, ch)
        load_cache(vc_in, vbuf, sem_v, 0, ch)
    load_second(0)

    in_l.wait()
    in_i.wait()
    eye_b = (lax.broadcasted_iota(jnp.int32, (B, B), 0) == lax.broadcasted_iota(jnp.int32, (B, B), 1))
    lcol = jnp.sum(jnp.where(eye_b, lrow[...].astype(F32), 0.0), axis=1, keepdims=True)
    lenb[...] = jnp.broadcast_to(lcol, (B, D))
    ang = lcol * inv[...]
    cosb[...] = jnp.cos(ang)
    half = lax.broadcasted_iota(jnp.int32, (B, D), 1) < D // 2
    sn = jnp.sin(ang)
    sinb[...] = jnp.where(half, -sn, sn)

    def stage_in(l, chunks):
        span = pl.ds(chunks[0] * R, R * len(chunks))
        scales = []
        for ch in chunks:
            if l > 0 or ch == 0:
                arrived("h", ch)
                arrived("s", ch)
            row = ssb[l, 0, ch]
            for slot in range(1, NX * NY):
                row = row + ssb[l, slot, ch]
            col = jnp.sum(jnp.where(eye, row, 0.0), axis=1, keepdims=True)
            scales.append(lax.rsqrt(col / E + EPS))
        r = jnp.concatenate(scales, axis=0)
        if 0 in chunks:
            if l == 0:
                ref = gg.at[pl.ds(0, NY - 1)]
                pltpu.make_async_copy(ref, ref, g_sem.at[1]).wait()
                pltpu.make_async_copy(ref, ref, g_sem.at[0]).wait()
            need_w(l, 0)
            need_w(l, 1)
        xs = []
        for j in range(NY):
            gj = gg[j, pl.ds(l, 1), :].astype(F32)
            xs.append((hg[l, j, span, :].astype(F32) * r * gj).astype(BF16))
        x = jnp.concatenate(xs, axis=1)
        xbuf[span, :] = x
        for n in range(2):
            acc = _dot(x, wqkv[l, 0, :, pl.ds(n * 256, 256)])
            for m in range(2):
                a = acc[:, m * D:(m + 1) * D]
                qf[2 * n + m, span, :] = a
                qb[l, 2 * n + m, span, :] = a.astype(BF16)

    def send_q(l, ch):
        rows = pl.ds(ch * R, R)
        tos = [lax.rem(xi + d, NX) for d in range(NX)]
        exchange("q", l, ch, [(qb.at[l, tos[d], rows], qr.at[l, d - 1, rows], {"x": tos[d]}) for d in (2, 1, 3)],
                 qr.at[l, :, rows])

    def stage_in_rest(l, chunks):
        span = pl.ds(chunks[0] * R, R * len(chunks))
        x = xbuf[span, :]
        for t in range(2):
            for n in range(2):
                acc = _dot(x, wqkv[l, t + 1, :, pl.ds(n * 256, 256)])
                for cc in range(2):
                    a = acc[:, cc * D:(cc + 1) * D]
                    pf[cc, t, n, span, :] = a
                    pb[l, cc, t, n, span, :] = a.astype(BF16)
        for ch in chunks:
            rows = pl.ds(ch * R, R)
            exchange("kv", l, ch, [(pb.at[l, 1 - c, :, :, rows], rq.at[l, :, :, rows], {"x": partner})],
                     rq.at[l, :, :, rows])
        for n in range(8):
            acc = _dot(x, win[l, :, pl.ds(n * 256, 256)])
            cols = pl.ds((n % 4) * 256, 256)
            uf[n // 4, span, cols] = acc
            ub[l, n // 4, span, cols] = acc.astype(BF16)
        for ch in chunks:
            rows = pl.ds(ch * R, R)
            exchange("u", l, ch, [(ub.at[l, 1 - c, rows], ur.at[l, rows], {"x": partner})], ur.at[l, rows])
        if nch - 1 in chunks and l + 1 < L:
            load_first(l + 1)

    def reduce_kv(l, ch):
        rows = pl.ds(ch * R, R)
        arrived("kv", ch)
        for t in range(2):
            for n in range(2):
                s = pf[c, t, n, rows, :] + rq[l, t, n, rows, :].astype(F32)
                sf[n, t, rows, :] = s
                sb[l, n, t, rows, :] = s.astype(BF16)
        exchange("kvx", l, ch, [(sb.at[l, 1 - xc, :, rows], xr.at[l, :, rows], {"x": across})], xr.at[l, :, rows])

    u_done = {}

    def reduce_u(l, ch):
        pieces = ORDER.count(f"RU{'AB'[ch]}{l}")
        piece = u_done.get((l, ch), 0)
        u_done[l, ch] = piece + 1
        if piece == 0:
            arrived("u", ch)
        rows = pl.ds(ch * R + piece * (R // pieces), R // pieces)
        us = uf[c, rows, :] + ur[l, rows, :].astype(F32)
        usf[rows, :] = us
        usb[l, rows, :] = us.astype(BF16)
        exchange("ux", l, ch, [(usb.at[l, rows], ux.at[l, rows], {"x": across})], ux.at[l, pl.ds(ch * R, R)],
                 first=piece == 0)

    def rope(t, rows):
        tf = t.astype(F32)
        return (tf * cosb[rows, :] + pltpu.roll(tf, D // 2, 1) * sinb[rows, :]).astype(BF16)

    def stage_q(l, ch):
        rows = pl.ds(ch * R, R)
        arrived("q", ch)
        q = qf[xi, rows, :]
        for d in range(NX - 1):
            q = q + qr[l, d, rows, :].astype(F32)
        qv[rows, :] = rope(q.astype(BF16), rows)

    rowid = lax.broadcasted_iota(jnp.int32, (G, D), 0)
    pos = lax.broadcasted_iota(jnp.int32, (R, S), 1).astype(F32)
    scale = D ** -0.5

    ready, flipped, scored = set(), {}, {}

    def need_keys(l, ch):
        if (l, ch) not in ready:
            ready.add((l, ch))
            need_cache(kbuf, sem_k, ch)

    def transpose(l, ch):
        need_keys(l, ch)
        g = flipped.get((l, ch), 0)
        flipped[l, ch] = g + 1
        for b in range(ch * R + g * G, ch * R + (g + 1) * G):
            for j in range(S // D):
                kbuf[b, pl.ds(j * D, D), :] = kbuf[b, pl.ds(j * D, D), :].T

    def scores(l, ch):
        need_keys(l, ch)
        first = scored.get((l, ch), 0)
        scored[l, ch] = first + gpc // 2
        for g in range(first, first + gpc // 2):
            base = ch * R + g * G
            rows = pl.ds(base, G)
            q = qv[rows, :].astype(F32)
            s = jnp.zeros((G, S), F32)
            for i in range(0, G, 2):
                lhs = jnp.concatenate([jnp.where(rowid == i, q, 0.0), jnp.where(rowid == i + 1, q, 0.0)],
                                      axis=1).astype(BF16)
                if g < flipped.get((l, ch), 0):
                    keys = [jnp.concatenate([kbuf[base + i + e, pl.ds(j * D, D), :] for j in range(S // D)], axis=1)
                            for e in range(2)]
                    s = s + _dot(lhs, jnp.concatenate(keys, axis=0))
                else:
                    s = s + _dot_t(lhs, jnp.concatenate([kbuf[base + i], kbuf[base + i + 1]], axis=1))
            sbuf[rows, :] = s
        if scored[l, ch] == gpc and l + 1 < L:
            load_cache(kc_in, kbuf, sem_k, l + 1, ch)

    def softmax(l, ch):
        rows = pl.ds(ch * R, R)
        s = jnp.where(pos < lenb[rows, :][:, :1], sbuf[rows, :] * scale, -jnp.inf)
        m = jnp.max(s, axis=1, keepdims=True)
        p = jnp.exp(s - m)
        pbuf[rows, :] = p.astype(BF16)
        mbuf[rows, :] = jnp.broadcast_to(m, (R, D))
        dbuf[rows, :] = jnp.broadcast_to(jnp.sum(p, axis=1, keepdims=True), (R, D))

    def values(l, ch):
        need_cache(vbuf, sem_v, ch)
        for g in range(gpc):
            base = ch * R + g * G
            rows = pl.ds(base, G)
            p = pbuf[rows, :]
            o = jnp.zeros((G, D), F32)
            for i in range(0, G, 2):
                t = _dot(p, jnp.concatenate([vbuf[base + i], vbuf[base + i + 1]], axis=1))
                o = o + jnp.where(rowid == i, t[:, :D], jnp.where(rowid == i + 1, t[:, D:], 0.0))
            obuf[rows, :] = o

    def load_values(l, ch):
        load_cache(vc_in, vbuf, sem_v, l + 1, ch)

    def stage_kv(l, ch):
        rows = pl.ds(ch * R, R)
        arrived("kvx", ch)
        k = rope((sf[xc, 0, rows, :] + xr[l, 0, rows, :].astype(F32)).astype(BF16), rows)
        v = (sf[xc, 1, rows, :] + xr[l, 1, rows, :].astype(F32)).astype(BF16)
        k_out[l, rows, :] = k
        v_out[l, rows, :] = v
        s_new = jnp.sum(qv[rows, :].astype(F32) * k.astype(F32), axis=1, keepdims=True) * scale
        m_c = mbuf[rows, :]
        m = jnp.maximum(m_c, s_new)
        a = jnp.exp(m_c - m)
        p_new = jnp.exp(s_new - m)
        o = (a * obuf[rows, :] + p_new * v.astype(F32)) / (a * dbuf[rows, :] + p_new)
        og[l, xi, rows, :] = o.astype(BF16)

    def send_o(l, ch):
        rows = pl.ds(ch * R, R)
        exchange("o", l, ch, [(og.at[l, xi, rows], og.at[l, xi, rows], {"x": lax.rem(xi + d, NX)}) for d in (2, 1, 3)],
                 og.at[l, pl.ds(0, NX - 1), rows])

    def stage_f(l, ch):
        rows = pl.ds(ch * R, R)
        arrived("ux", ch)
        u = (usf[rows, :] + ux[l, rows, :].astype(F32)).astype(BF16)
        fb[l, c, rows, :] = jax.nn.gelu(u.astype(F32), approximate=True).astype(BF16)
        exchange("f", l, ch, [(fb.at[l, c, rows], fb.at[l, c, rows], {"x": partner})], fb.at[l, 0, rows])

    def stage_mlp(l, ch):
        rows = pl.ds(ch * R, R)
        arrived("f", ch)
        if ch == 0:
            need_w(l, 3)
        f = jnp.concatenate([fb[l, 0, rows, :], fb[l, 1, rows, :]], axis=1)
        for n in range(2):
            acc = _dot(f, wout[l, :, pl.ds(n * 256, 256)])
            zf[2 * n, rows, :] = acc[:, :D]
            zf[2 * n + 1, rows, :] = acc[:, D:]

    def stage_out(l, ch):
        rows = pl.ds(ch * R, R)
        arrived("o", ch)
        if ch == 0:
            need_w(l, 2)
        o = jnp.concatenate([og[l, j, rows, :] for j in range(NX)], axis=1)
        for n in range(2):
            acc = _dot(o, wo[l, :, pl.ds(n * 256, 256)])
            for m in range(2):
                a = acc[:, m * D:(m + 1) * D] + zf[2 * n + m, rows, :]
                zf[2 * n + m, rows, :] = a
                zb[l, 2 * n + m, rows, :] = a.astype(BF16)
        tos = [lax.rem(yi + d, NY) for d in range(NY)]
        exchange("y", l, ch, [(zb.at[l, tos[d], rows], zr.at[l, d - 1, rows], {"yz": tos[d]}) for d in (3, 1, 2)],
                 zr.at[l, :, rows])
        if ch == nch - 1 and l + 1 < L:
            load_second(l + 1)

    def stage_h(l, ch):
        rows = pl.ds(ch * R, R)
        arrived("y", ch)
        y = zf[yi, rows, :]
        for d in range(NY - 1):
            y = y + zr[l, d, rows, :].astype(F32)
        hn = (hg[l, yi, rows, :].astype(F32) + y.astype(BF16).astype(F32)).astype(BF16)
        if l + 1 < L:
            hg[l + 1, yi, rows, :] = hn
            stats(l + 1, ch, hn.astype(F32))
            send_h(l + 1, ch, rows, pl.ds(ch, 1))
        else:
            h_out[rows, :] = hn

    stages = dict(IN=stage_in, SQ=send_q, JN=stage_in_rest, RKV=reduce_kv, RU=reduce_u, Q=stage_q, QK=scores, X=transpose, KV=stage_kv, SM=softmax, PV=values, LV=load_values,
                  SO=send_o, F=stage_f, MLP=stage_mlp, OUT=stage_out, H=stage_h)
    for step in ORDER:
        with jax.named_scope(step):
            chunks = range(nch) if step[-2] == "*" else ("AB".index(step[-2]),)
            stages[step[:-2]](int(step[-1]), chunks if step[:2] in ("IN", "JN") else chunks[0])
    for n, ch in list(open_sends):
        drain(n, ch)


def _tail(h_in, k_in, v_in, h_out, k_out, v_out, sem):
    cps = [pltpu.make_async_copy(a, o, sem.at[n])
           for n, (a, o) in enumerate(((k_in, k_out), (v_in, v_out), (h_in, h_out)))]
    for cp in cps:
        cp.start()
    for cp in cps:
        cp.wait()


def solution(mesh):
    nch = 2
    act = P(None, ('x', 'yz'))
    w_first = P(None, 'x', 'yz')
    w_second = P(None, 'yz', 'x')
    cache = P(None, None, ('yz', 'x'), None, None)
    new = P(None, None, ('yz', 'x'), None)
    inv_half = 10000.0 ** (-np.arange(D // 2, dtype=np.float64) / (D // 2))
    inv_np = np.concatenate([inv_half, inv_half]).astype(np.float32)[None]

    def body(h, g, wq, wk, wv, w_in, wo, w_out, kc, vc, lens):
        any_spec = pl.BlockSpec(memory_space=pl.ANY)
        vm_spec = pl.BlockSpec(memory_space=pltpu.VMEM)
        shapes = ((B, D), (L, B, D), (L, B, D))
        vm = pltpu.VMEM
        dma = pltpu.SemaphoreType.DMA
        scratch = [
            vm((B, S, D), BF16), vm((B, S, D), BF16),
            vm((L, 3, 512, 512), BF16), vm((L, 512, 2048), BF16), vm((L, 512, 512), BF16), vm((L, 2048, 512), BF16),
            vm((NY, L, D), BF16), vm((1, B), jnp.int32), vm((1, D), F32),
            vm((B, D), F32), vm((B, D), F32), vm((B, D), F32),
            vm((L, NY, B, D), BF16),
            vm((L, NX * NY, nch, 1, B), F32),
            vm((NX, B, D), F32),
            vm((L, NX, B, D), BF16),
            vm((L, NX - 1, B, D), BF16),
            vm((2, 2, 2, B, D), F32),
            vm((L, 2, 2, 2, B, D), BF16),
            vm((L, 2, 2, B, D), BF16),
            vm((2, 2, B, D), F32),
            vm((L, 2, 2, B, D), BF16),
            vm((L, 2, B, D), BF16),
            vm((2, B, 1024), F32),
            vm((L, 2, B, 1024), BF16),
            vm((L, B, 1024), BF16),
            vm((B, 1024), F32),
            vm((L, B, 1024), BF16),
            vm((L, B, 1024), BF16),
            vm((L, 2, B, 1024), BF16),
            vm((L, NX, B, D), BF16),
            vm((NY, B, D), F32),
            vm((L, NY, B, D), BF16),
            vm((L, NY - 1, B, D), BF16),
            vm((B, NY * D), BF16), vm((B, D), BF16), vm((B, D), F32),
            vm((B, S), F32), vm((B, S), BF16), vm((B, D), F32), vm((B, D), F32),
            dma((4,)), dma((4,)), dma((nch,)), dma((nch,)), dma((2,)),
            dma((3, nch)), dma((len(KINDS), nch)),
        ]
        h_new, k_new, v_new = pl.pallas_call(
            functools.partial(_kernel, nch),
            out_shape=tuple(vm(n, BF16) for n in shapes),
            in_specs=[any_spec] * 12,
            out_specs=(vm_spec,) * 3,
            scratch_shapes=scratch,
            compiler_params=pltpu.CompilerParams(collective_id=0, has_side_effects=True,
                                                 vmem_limit_bytes=66_000_000),
            name="decode_step",
        )(h, g, wq, wk, wv, w_in, wo, w_out, kc.reshape(L, B, S, D), vc.reshape(L, B, S, D),
          lens.reshape(1, B), jnp.asarray(inv_np))
        h_new, k_new, v_new = pl.pallas_call(
            _tail,
            out_shape=tuple(jax.ShapeDtypeStruct(n, BF16) for n in shapes),
            in_specs=[vm_spec] * 3,
            out_specs=(any_spec,) * 3,
            scratch_shapes=[dma((3,))],
            name="results",
        )(*(pltpu.with_memory_space_constraint(a, pltpu.VMEM) for a in (h_new, k_new, v_new)))
        return h_new, k_new.reshape(L, B, 1, D), v_new.reshape(L, B, 1, D)

    return jax.shard_map(
        body, mesh=mesh,
        in_specs=(act, act, w_first, w_first, w_first, w_first, w_second, w_second, cache, cache, P(None)),
        out_specs=(act, new, new), check_vma=False)
```

profile of v0, /device:TPU:0, one launch (start us, length us, event | category | flops | bytes accessed | tf_op | source)
XLA Modules:
  0.0 45.8 jit_solution(2206319950457312971)
XLA Ops:
  0.6 44.4 %decode_step.1 = (bf16[128,128]{1,0:T(8,128)(2,1)S(1)}, bf16[2,128,128]{2,1,0:T(8,128)(2,1)S(1)}, bf16[2,128,128]{2,1,0:T(8,128)(2,1)S(1)}) custom-call(bf16[128,128]{1,0:T(8,128)(2,1)} %h_in.1, bf16[2,128]{1,0:T(2,128)(2,1)} %g_in.1, bf16[2,512,512]{2,1,0:T(8,128)(2,1)} %wq_in.1, bf16[2,512,512]{2,1,0:T(8,128)(2,1)} %wk_in.1, bf16[2,512,512]{2,1,0:T(8,128)(2,1)} %wv_in.1, ...), custom_call_target="tpu_custom_call" | custom-call | tf_op jit(solution)/shard_map/decode_step/pallas_call | solution.py:465
  45.0 0.7 %results.1 = (bf16[128,128]{1,0:T(8,128)(2,1)}, bf16[2,128,128]{2,1,0:T(8,128)(2,1)}, bf16[2,128,128]{2,1,0:T(8,128)(2,1)}) custom-call(bf16[128,128]{1,0:T(8,128)(2,1)S(1)} %get-tuple-element.9.h_in, bf16[2,128,128]{2,1,0:T(8,128)(2,1)S(1)} %get-tuple-element.10.k_in, bf16[2,128,128]{2,1,0:T(8,128)(2,1)S(1)} %get-tuple-element.11.v_in), custom_call_target="tpu_custom_call" | custom-call | tf_op jit(solution)/shard_map/results/pallas_call | solution.py:476
where the time goes:
time: 46 us; the launch traced here: 45.8 us
  Pallas kernels  45 us (98%)
  between operations  0.8 us (2%)
    pallas_call x1, Pallas kernels, body(): pl.pallas_call(functools.partial(_kernel, nch), out_shape=tuple((vm(n, BF...  44.4 us

commit v1 on v0

--- a/solution.py
+++ b/solution.py
@@ -27,7 +27,7 @@
 KINDS = {k: n for n, k in enumerate(("s", "h", "q", "kv", "kvx", "u", "ux", "f", "o", "y"))}
 SENDS = {"s": 0, "h": 1, "q": 0, "kv": 1, "kvx": 1, "u": 2, "ux": 2, "f": 1, "o": 0, "y": 0}
 ORDER = ("IN*0 SQA0 SQB0 JN*0 XA0 RKVA0 XA0 RUA0 XA0 XA0 QA0 QKA0 QKA0 RKVB0 RUB0 SMA0 PVA0 KVA0 SOA0 RUB0 QB0 QKB0 QKB0 "
-         "FA0 SMB0 PVB0 KVB0 SOB0 MLPA0 OUTA0 XA1 FB0 XA1 XA1 MLPB0 OUTB0 XA1 HA0 XB1 LVA0 XB1 XB1 LVB0 XB1 HB0 INA1 SQA1 JNA1 "
+         "FA0 SMB0 PVB0 KVB0 SOB0 MLPA0 OUTA0 XA1 FB0 XA1 XA1 MLPB0 OUTB0 XA1 HA0 XB1 LVA0 XB1 XB1 LVB0 HB0 XB1 INA1 SQA1 JNA1 "
          "RKVA1 RUA1 INB1 SQB1 RUA1 JNB1 QA1 QKA1 QKA1 RKVB1 RUB1 SMA1 PVA1 KVA1 SOA1 QB1 QKB1 QKB1 SMB1 PVB1 KVB1 SOB1 FA1 "
          "MLPA1 FB1 OUTA1 MLPB1 OUTB1 HA1 HB1").split()
 

time: 46 us -> 46 us (level)
  no operation moved by 1% of the time
where the time goes in v1:
time: 46 us; the launch traced here: 45.8 us
  Pallas kernels  45 us (98%)
  between operations  0.8 us (2%)
    pallas_call x1, Pallas kernels, body(): pl.pallas_call(functools.partial(_kernel, nch), out_shape=tuple((vm(n, BF...  44.4 us

profile of v1, /device:TPU:0, one launch (start us, length us, event | category | flops | bytes accessed | tf_op | source)
XLA Modules:
  0.0 45.8 jit_solution(9145225282998042775)
XLA Ops:
  0.6 44.4 %decode_step.1 = (bf16[128,128]{1,0:T(8,128)(2,1)S(1)}, bf16[2,128,128]{2,1,0:T(8,128)(2,1)S(1)}, bf16[2,128,128]{2,1,0:T(8,128)(2,1)S(1)}) custom-call(bf16[128,128]{1,0:T(8,128)(2,1)} %h_in.1, bf16[2,128]{1,0:T(2,128)(2,1)} %g_in.1, bf16[2,512,512]{2,1,0:T(8,128)(2,1)} %wq_in.1, bf16[2,512,512]{2,1,0:T(8,128)(2,1)} %wk_in.1, bf16[2,512,512]{2,1,0:T(8,128)(2,1)} %wv_in.1, ...), custom_call_target="tpu_custom_call" | custom-call | tf_op jit(solution)/shard_map/decode_step/pallas_call | solution.py:465
  45.0 0.7 %results.1 = (bf16[128,128]{1,0:T(8,128)(2,1)}, bf16[2,128,128]{2,1,0:T(8,128)(2,1)}, bf16[2,128,128]{2,1,0:T(8,128)(2,1)}) custom-call(bf16[128,128]{1,0:T(8,128)(2,1)S(1)} %get-tuple-element.9.h_in, bf16[2,128,128]{2,1,0:T(8,128)(2,1)S(1)} %get-tuple-element.10.k_in, bf16[2,128,128]{2,1,0:T(8,128)(2,1)S(1)} %get-tuple-element.11.v_in), custom_call_target="tpu_custom_call" | custom-call | tf_op jit(solution)/shard_map/results/pallas_call | solution.py:476
